TPU v7x, 32 devices: a whole 2x2x4 slice. The times are simulated.
32 devices in a mesh: section: 8 (over z, y), fsdp: 4 (over x, core).
Axes of the slice: x: 2, y: 2, z: 4, core: 2. Of those that a mesh axis runs over, the one named last changes fastest.
Arguments:
- source_rows: bfloat16 [3072, 4096], P(('section', 'fsdp')), may hold values from -6 to 6
- target_rows: bfloat16 [1024, 4096], P('section'), may hold values from -6 to 6
- attn_weights: bfloat16 [8, 4, 4096, 3072], P('section', None, None, 'fsdp'), may hold values from -3.76875 to 3.76875
- gains: float32 [8, 4096], P('section'), may hold values from 0.25 to 1.75
- lengths: int32 [8], P('section'), may hold values from 192 to 384
Outputs:
- source_next: bfloat16 [3072, 4096], P(('section', 'fsdp'))
- target_next: bfloat16 [1024, 4096], P('section')
Inputs may be any that keep to these rules, and one draw needn't show every extreme that they name: Keys at positions lengths[s] and beyond are padding.
All inputs are finite; a program needn't handle non-finite values.
Results may differ from a plain program's by a relative error of at most 0.015.
The roundings to bfloat16 on the way count: a program that leaves them out, or rounds other values in their place, can miss the bound.
Values may be sent and summed in bfloat16 or wider, within the bound.
A program may use at most 128 MiB of HBM per device.

v0:
```python
import jax
import jax.numpy as jnp
from jax import lax
from jax.sharding import PartitionSpec as P

HEAD_DIM = 64


def shifted(value, axis, steps):
    count = lax.axis_size(axis)
    pairs = [(source, (source + steps) % count) for source in range(count)]
    return lax.ppermute(value, axis, pairs)


def rms_norm(block_rows, gain_row):
    widened = block_rows.astype(jnp.float32)
    inverse_rms = lax.rsqrt(jnp.mean(widened * widened, axis=-1, keepdims=True) + 1e-06)
    return (widened * inverse_rms * gain_row).astype(jnp.bfloat16)


def project(block_rows, weight):
    return jnp.dot(block_rows, weight, preferred_element_type=jnp.float32).astype(jnp.bfloat16)


def attend(queries, key_rows, values, length):
    query_count = queries.shape[0]
    key_count = key_rows.shape[0]
    head_count = queries.shape[1] // HEAD_DIM
    query_heads = queries.reshape(query_count, head_count, HEAD_DIM)
    key_heads = key_rows.reshape(key_count, head_count, HEAD_DIM)
    value_heads = values.reshape(key_count, head_count, HEAD_DIM)
    scores = (
        jnp.einsum("qhc,khc->hqk", query_heads, key_heads, preferred_element_type=jnp.float32)
        * 0.125
    )
    key_valid = jnp.arange(key_count, dtype=jnp.int32) < length
    scores = jnp.where(key_valid[None, None, :], scores, -1000000000.0)
    row_max = jnp.max(scores, axis=-1, keepdims=True)
    expo = jnp.exp(scores - row_max)
    soft = (expo / jnp.sum(expo, axis=-1, keepdims=True)).astype(jnp.bfloat16)
    context = jnp.einsum("hqk,khc->qhc", soft, value_heads, preferred_element_type=jnp.float32)
    return context.reshape(query_count, head_count * HEAD_DIM).astype(jnp.bfloat16)


def out_partial(context, out_weight):
    return lax.dot_general(
        context, out_weight, (((1,), (1,)), ((), ())), preferred_element_type=jnp.float32
    )


def local(source_rows, target_rows, attn_weights, gains, lengths):
    section_index = lax.axis_index("section")
    encoder_section = section_index < lax.axis_size("section") // 2
    weights = attn_weights[0]
    gain_row = gains[0]
    length = lengths[0]
    source_whole = lax.all_gather(source_rows, "fsdp", axis=0, tiled=True)

    def encoder_work(whole_rows, target_block):
        normed = rms_norm(whole_rows, gain_row)
        context = attend(
            project(normed, weights[0]),
            project(normed, weights[1]),
            project(normed, weights[2]),
            length,
        )
        return (out_partial(context, weights[3]), jnp.zeros(target_block.shape, jnp.float32))

    def decoder_work(whole_rows, target_block):
        normed = rms_norm(target_block, gain_row)
        context = attend(
            project(normed, weights[0]),
            project(whole_rows, weights[1]),
            project(whole_rows, weights[2]),
            length,
        )
        return (jnp.zeros(whole_rows.shape, jnp.float32), out_partial(context, weights[3]))

    source_terms, target_terms = lax.cond(
        encoder_section, encoder_work, decoder_work, source_whole, target_rows
    )
    source_sum = lax.psum_scatter(
        source_terms.astype(jnp.bfloat16), "fsdp", scatter_dimension=0, tiled=True
    ).astype(jnp.float32)
    source_new = (source_rows.astype(jnp.float32) + source_sum).astype(jnp.bfloat16)
    target_sum = lax.psum(target_terms.astype(jnp.bfloat16), "fsdp").astype(jnp.float32)
    target_new = (target_rows.astype(jnp.float32) + target_sum).astype(jnp.bfloat16)
    source_next, target_next = shifted((source_new, target_new), "section", 1)
    return (source_next, target_next)


def solution(mesh):
    in_specs = (
        P(("section", "fsdp"), None),
        P("section", None),
        P("section", None, None, "fsdp"),
        P("section", None),
        P("section"),
    )
    out_specs = (P(("section", "fsdp"), None), P("section", None))
    return jax.shard_map(local, mesh=mesh, in_specs=in_specs, out_specs=out_specs, check_vma=False)
```

profile of v0, /device:TPU:0, one launch (start us, length us, event | category | flops | bytes accessed | tf_op | source)
XLA Modules:
  0.0 194.1 jit_solution(7510881435808563548)
XLA Ops:
  7.2 0.7 all-gather.2.cloned.1.call-update
  7.9 32.8 %all-gather.2.cloned.1.call-done = bf16[384,4096]{1,0:T(8,128)(2,1)} async-done(((bf16[96,4096]{1,0:T(8,128)(2,1)}), bf16[384,4096]{1,0:T(8,128)(2,1)}) %all-gather.2.cloned.1.call-update) | async-done | bytes 3145744 | tf_op jit(solution)/shard_map/all_gather | solution.py:57
  40.8 46.0 %conditional.1 = (bf16[384,4096]{1,0:T(8,128)(2,1)S(1)}, bf16[128,4096]{1,0:T(8,128)(2,1)}) conditional(s32[]{:T(128)} %convert_element_type.82, (bf16[4,4096,768]{2,1,0:T(8,128)(2,1)}, bf16[384,4096]{1,0:T(8,128)(2,1)}, s32[]{:T(128)}, bf16[128,4096]{1,0:T(8,128)(2,1)}, f32[1,4096]{1,0:T(1,128)}) %tuple.31, (bf16[384,4096]{1,0:T(8,128)(2,1)}, ...), branch_computations={%region_0.4_spmd, %region_4.8_spmd} | conditional | flops 10152052736 | bytes 77100880 | solution.py:79
  40.8 2.6 %fusion.39 = f32[384]{0:T(512)S(1)} fusion(bf16[384,4096]{1,0:T(8,128)(2,1)} %get-tuple-element.23), kind=kLoop, calls=%fused_computation.43 | loop fusion | flops 4718208 | bytes 3147264 | tf_op jit(solution)/shard_map/cond/branch_1_fun/reduce_sum | solution.py:17
  43.4 7.4 %fusion.63 = bf16[384,768]{1,0:T(8,128)(2,1)} fusion(bf16[4,4096,768]{2,1,0:T(8,128)(2,1)} %get-tuple-element.25, bf16[384,4096]{1,0:T(8,128)(2,1)} %get-tuple-element.23, f32[4096]{0:T(1024)} %bitcast.73, f32[384]{0:T(512)S(1)} %add_rsqrt_fusion.1), kind=kOutput, calls=%fused_computation.65 | convolution fusion | flops 2422505472 | bytes 10044928 | tf_op jit(solution)/shard_map/cond/branch_1_fun/dot_general | solution.py:22
  50.8 2.1 %copy.18 = bf16[384,768]{0,1:T(8,128)(2,1)} copy(bf16[384,768]{1,0:T(8,128)(2,1)} %fusion.63) | data formatting | bytes 1179648 | tf_op jit(solution)/shard_map/cond/branch_1_fun/convert_element_type | solution.py:22
  52.9 6.3 %fusion.66 = bf16[384,768]{1,0:T(8,128)(2,1)} fusion(bf16[4,4096,768]{2,1,0:T(8,128)(2,1)} %get-tuple-element.25, bf16[384,4096]{1,0:T(8,128)(2,1)S(1)} %copy-done.2, f32[4096]{0:T(1024)S(1)} %bitcast.74, f32[384]{0:T(512)S(1)} %add_rsqrt_fusion.1), kind=kOutput, calls=%fused_computation.66 | convolution fusion | flops 2422505472 | bytes 10044928 | tf_op jit(solution)/shard_map/cond/branch_1_fun/dot_general | solution.py:22
  59.2 2.1 %copy.19 = bf16[384,768]{0,1:T(8,128)(2,1)} copy(bf16[384,768]{1,0:T(8,128)(2,1)} %fusion.66) | data formatting | bytes 1179648 | tf_op jit(solution)/shard_map/cond/branch_1_fun/convert_element_type | solution.py:22
  62.0 7.0 %fusion.77 = (f32[12,384]{1,0:T(8,128)S(1)}, f32[12,384,384]{1,2,0:T(8,128)}) fusion(pred[384]{0:T(512)(128)(4,1)S(1)} %iota_compare_fusion.1, bf16[384,12,64]{0,2,1:T(8,128)(2,1)} %bitcast.64, bf16[384,12,64]{0,2,1:T(8,128)(2,1)} %bitcast.66), kind=kOutput, calls=%fused_computation.75 | convolution fusion | flops 233570688 | bytes 8276352 | tf_op jit(solution)/shard_map/cond/branch_1_fun/sub | solution.py:39
  68.9 6.3 %fusion.60 = bf16[384,768]{1,0:T(8,128)(2,1)} fusion(bf16[4,4096,768]{2,1,0:T(8,128)(2,1)} %get-tuple-element.25, bf16[384,4096]{1,0:T(8,128)(2,1)S(1)} %copy-done.2, f32[4096]{0:T(1024)S(1)} %bitcast.75, f32[384]{0:T(512)S(1)} %add_rsqrt_fusion.1), kind=kOutput, calls=%fused_computation.64 | convolution fusion | flops 2422505472 | bytes 10044928 | tf_op jit(solution)/shard_map/cond/branch_1_fun/dot_general | solution.py:22
  75.2 1.4 copy.17
  76.5 3.7 %fusion.59 = bf16[12,64,384]{2,1,0:T(8,128)(2,1)S(1)} fusion(bf16[384,12,64]{0,2,1:T(8,128)(2,1)S(1)} %bitcast.68, f32[12,384,384]{1,2,0:T(8,128)} %get-tuple-element.36, f32[12,384]{1,0:T(8,128)S(1)} %get-tuple-element.35), kind=kOutput, calls=%fused_computation.63 | convolution fusion | flops 230326272 | bytes 8275968 | tf_op jit(solution)/shard_map/cond/branch_1_fun/hqk,khc->qhc/dot_general | solution.py:41
  80.3 5.4 %fusion.42 = bf16[384,4096]{1,0:T(8,128)(2,1)S(1)} fusion(bf16[384,768]{0,1:T(8,128)(2,1)S(1)} %bitcast.76, bf16[4,4096,768]{2,1,0:T(8,128)(2,1)} %get-tuple-element.25), kind=kOutput, calls=%fused_computation.46 | convolution fusion | flops 2415919104 | bytes 10027008 | tf_op jit(solution)/shard_map/cond/branch_1_fun/dot_general | solution.py:46
  85.7 1.1 broadcast.57
  86.9 1.6 copy-done
  88.5 32.9 %all-reduce.2.cloned.1.call-done = bf16[128,4096]{1,0:T(8,128)(2,1)} async-done(((bf16[128,4096]{1,0:T(8,128)(2,1)}), bf16[128,4096]{1,0:T(8,128)(2,1)}) %all-reduce.2.cloned.1.call-update) | async-done | bytes 1048592 | tf_op jit(solution)/shard_map/psum | solution.py:86
  121.4 1.8 add_convert_fusion
  123.2 1.5 collective-permute-start.1
  124.7 37.6 %reduce-scatter.2.cloned.1.call-done = bf16[96,4096]{1,0:T(8,128)(2,1)} async-done(((bf16[384,4096]{1,0:T(8,128)(2,1)}), bf16[96,4096]{1,0:T(8,128)(2,1)}) %reduce-scatter.2.cloned.1.call-update) | async-done | bytes 786448 | tf_op jit(solution)/shard_map/reduce_scatter | solution.py:82
  162.3 1.6 add_convert_fusion.1
  163.9 1.5 collective-permute-start
  165.4 20.3 %collective-permute-done = bf16[96,4096]{1,0:T(8,128)(2,1)S(1)} collective-permute-done((bf16[96,4096]{1,0:T(8,128)(2,1)S(1)}, bf16[96,4096]{1,0:T(8,128)(2,1)S(1)}, u32[]{:S(2)}, u32[]{:S(2)}) %collective-permute-start) | collective-permute-done | bytes 786464 | tf_op jit(solution)/shard_map/ppermute | solution.py:12
  185.8 0.9 copy.29
  186.6 1.0 copy.30
  (13 shorter events, 0.8 us)
Async XLA Ops:
  7.2 33.6 %all-gather.2.cloned.1.call-start = ((), (), s32[]{:S(2)}) async-start(), calls=%async_computation.1 | async-start | bytes 3932160 | tf_op jit(solution)/shard_map/all_gather | solution.py:57
  7.9 113.5 %all-reduce.2.cloned.1.call-start = ((), (), s32[]{:S(2)}) async-start(), calls=%async_computation.3 | async-start | bytes 2097152 | tf_op jit(solution)/shard_map/psum | solution.py:86
  43.4 9.5 %copy-start.2 = (bf16[384,4096]{1,0:T(8,128)(2,1)S(1)}, bf16[384,4096]{1,0:T(8,128)(2,1)}, u32[]{:S(2)}) copy-start(bf16[384,4096]{1,0:T(8,128)(2,1)} %get-tuple-element.23) | copy-start | bytes 9437188 | tf_op jit(solution)/shard_map/cond
  43.4 9.5 %copy-start.3 = (f32[1,4096]{1,0:T(1,128)S(1)}, f32[1,4096]{1,0:T(1,128)}, u32[]{:S(2)}) copy-start(f32[1,4096]{1,0:T(1,128)} %get-tuple-element.24) | copy-start | bytes 49156 | tf_op jit(solution)/shard_map/cond
  86.8 1.7 copy-start
  86.8 75.5 %reduce-scatter.2.cloned.1.call-start = ((), (), s32[]{:S(2)}) async-start(), calls=%async_computation.2 | async-start | bytes 3932160 | tf_op jit(solution)/shard_map/reduce_scatter | solution.py:82
  123.2 42.2 %collective-permute-start.1 = (bf16[128,4096]{1,0:T(8,128)(2,1)S(1)}, bf16[128,4096]{1,0:T(8,128)(2,1)S(1)}, u32[]{:S(2)}, u32[]{:S(2)}) collective-permute-start(bf16[128,4096]{1,0:T(8,128)(2,1)S(1)} %add_convert_fusion), channel_id=1, source_target_pairs={{0,4},{4,8},{8,12},{12,16},{16,20},{20,24},{24,28},{28,0},{1,5},{5... | collective-permute-start | bytes 3145736 | tf_op jit(solution)/shard_map/ppermute | solution.py:12
  163.9 21.9 %collective-permute-start = (bf16[96,4096]{1,0:T(8,128)(2,1)S(1)}, bf16[96,4096]{1,0:T(8,128)(2,1)S(1)}, u32[]{:S(2)}, u32[]{:S(2)}) collective-permute-start(bf16[96,4096]{1,0:T(8,128)(2,1)S(1)} %add_convert_fusion.1), channel_id=1, source_target_pairs={{0,4},{4,8},{8,12},{12,16},{16,20},{20,24},{24,28},{28,0},{1,5},{5... | collective-permute-start | bytes 2359304 | tf_op jit(solution)/shard_map/ppermute | solution.py:12
Sparse Core Ops, SparseCore 0:
  9.5 31.2 all-gather.1
  86.9 34.4 all-reduce.1
  123.9 38.3 reduce-scatter.1
where the time goes:
time: 195 us; the launch traced here: 194 us
  waiting for transfers between devices  124 us (64%)
  matrix products  36 us (18%)
  between operations  13.8 us (7%)
  local copies, waits for them, and re-layouts  10.1 us (5%)
  other arithmetic  6.59 us (3%)
  starting transfers between devices  3.17 us (2%)
    reduce_scatter x1, waiting for transfers between devices, local(): lax.psum_scatter(source_terms.astype(jnp.bfloat16), 'fsdp', scatter_dimen...  37.6 us
    psum x1, waiting for transfers between devices, local(): lax.psum(target_terms.astype(jnp.bfloat16), 'fsdp').astype(jnp.float32)  32.9 us
    all_gather x1, waiting for transfers between devices, local(): source_whole = lax.all_gather(source_rows, 'fsdp', axis=0, tiled=True)  32.8 us
    ppermute x2, waiting for transfers between devices, shifted(): return lax.ppermute(value, axis, pairs)  20.3 us
    dot_general x3, matrix products, project(): jnp.dot(block_rows, weight, preferred_element_type=jnp.float32)  19.9 us
    sub x1, matrix products, attend(): expo = jnp.exp(scores - row_max)  6.96 us
    convert_element_type x3, local copies, waits for them, and re-layouts, project(): jnp.dot(block_rows, weight, preferred_element_type=jnp.float32)  5.62 us
    dot_general x1, matrix products, out_partial(): lax.dot_general(context, out_weight, (((1,), (1,)), ((), ())), preferred_...  5.45 us
  transfers between devices with their start and end apart: 5, of which 4 were waited for; matrix products, arithmetic and copies ran while one was open for 2% of the time, Pallas kernels for 0%

commit v1 on v0

--- a/solution.py
+++ b/solution.py
@@ -54,7 +54,14 @@
     weights = attn_weights[0]
     gain_row = gains[0]
     length = lengths[0]
-    source_whole = lax.all_gather(source_rows, "fsdp", axis=0, tiled=True)
+    size = lax.axis_size("fsdp")
+    hops = [(i, (i + 1) % size) for i in range(size)]
+    parts = [source_rows]
+    for stride in range(1, size):
+        parts = [lax.ppermute(parts[0], "fsdp", hops), *parts]
+    result = jnp.concatenate(parts, axis=0)
+    offset = (lax.axis_index("fsdp") + 1) * parts[-1].shape[0]
+    source_whole = jnp.roll(result, offset, axis=0)
 
     def encoder_work(whole_rows, target_block):
         normed = rms_norm(whole_rows, gain_row)

time: 195 us -> 199 us (1.021)
  waiting for transfers between devices: 124 us -> 129 us
  other arithmetic: 6.59 us -> 4.46 us
    ppermute x0 -> x3, waiting for transfers between devices: none -> 34.6 us  [local(): parts = [lax.ppermute(parts[0], 'fsdp', hops), *parts]]
    all_gather x1 -> x0, waiting for transfers between devices: 32.8 us -> none  [local(): source_whole = lax.all_gather(source_rows, 'fsdp', axis=0, tiled=True)]
    psum x1, waiting for transfers between devices: 32.9 us -> 35.7 us  [local(): lax.psum(target_terms.astype(jnp.bfloat16), 'fsdp').astype(jnp.float32)]
  transfers between devices with their start and end apart: 5 -> 7, of which waited for: 4 -> 6; matrix products, arithmetic and copies ran while one was open for 2% -> 2% of each run, Pallas kernels for 0% -> 0%
where the time goes in v1:
time: 199 us; the launch traced here: 198 us
  waiting for transfers between devices  129 us (65%)
  matrix products  36.3 us (18%)
  between operations  14.2 us (7%)
  local copies, waits for them, and re-layouts  10.3 us (5%)
  other arithmetic  4.46 us (2%)
  starting transfers between devices  3.72 us (2%)
    reduce_scatter x1, waiting for transfers between devices, local(): lax.psum_scatter(source_terms.astype(jnp.bfloat16), 'fsdp', scatter_dimen...  37.6 us
    psum x1, waiting for transfers between devices, local(): lax.psum(target_terms.astype(jnp.bfloat16), 'fsdp').astype(jnp.float32)  35.7 us
    ppermute x3, waiting for transfers between devices, local(): parts = [lax.ppermute(parts[0], 'fsdp', hops), *parts]  34.6 us
    ppermute x2, waiting for transfers between devices, shifted(): return lax.ppermute(value, axis, pairs)  20.3 us
    dot_general x3, matrix products, project(): jnp.dot(block_rows, weight, preferred_element_type=jnp.float32)  18.8 us
    dot_general x1, matrix products, out_partial(): lax.dot_general(context, out_weight, (((1,), (1,)), ((), ())), preferred_...  7.12 us
    sub x1, matrix products, attend(): expo = jnp.exp(scores - row_max)  6.78 us
    convert_element_type x3, local copies, waits for them, and re-layouts, project(): jnp.dot(block_rows, weight, preferred_element_type=jnp.float32)  4.85 us
  transfers between devices with their start and end apart: 7, of which 6 were waited for; matrix products, arithmetic and copies ran while one was open for 2% of the time, Pallas kernels for 0%

profile of v1, /device:TPU:0, one launch (start us, length us, event | category | flops | bytes accessed | tf_op | source)
XLA Modules:
  0.0 198.0 jit_solution(8622282099075192465)
XLA Ops:
  7.8 11.8 %collective-permute-done = bf16[96,4096]{1,0:T(8,128)(2,1)S(1)} collective-permute-done((bf16[96,4096]{1,0:T(8,128)(2,1)}, bf16[96,4096]{1,0:T(8,128)(2,1)S(1)}, u32[]{:S(2)}, u32[]{:S(2)}) %collective-permute-start) | collective-permute-done | bytes 786464 | tf_op jit(solution)/shard_map/ppermute | solution.py:61
  19.6 11.4 %collective-permute-done.1 = bf16[96,4096]{1,0:T(8,128)(2,1)S(1)} collective-permute-done((bf16[96,4096]{1,0:T(8,128)(2,1)S(1)}, bf16[96,4096]{1,0:T(8,128)(2,1)S(1)}, u32[]{:S(2)}, u32[]{:S(2)}) %collective-permute-start.1) | collective-permute-done | bytes 786464 | tf_op jit(solution)/shard_map/ppermute | solution.py:61
  31.0 11.4 %collective-permute-done.2 = bf16[96,4096]{1,0:T(8,128)(2,1)S(1)} collective-permute-done((bf16[96,4096]{1,0:T(8,128)(2,1)S(1)}, bf16[96,4096]{1,0:T(8,128)(2,1)S(1)}, u32[]{:S(2)}, u32[]{:S(2)}) %collective-permute-start.2) | collective-permute-done | bytes 786464 | tf_op jit(solution)/shard_map/ppermute | solution.py:61
  42.6 1.2 constant_dynamic-update-slice_fusion.4
  45.0 43.7 %conditional.1 = (bf16[384,4096]{1,0:T(8,128)(2,1)}, bf16[128,4096]{1,0:T(8,128)(2,1)}) conditional(s32[]{:T(128)} %convert_element_type.82, (bf16[4,4096,768]{2,1,0:T(8,128)(2,1)}, bf16[384,4096]{1,0:T(8,128)(2,1)S(1)}, s32[]{:T(128)}, bf16[128,4096]{1,0:T(8,128)(2,1)S(1)}, f32[1,4096]{1,0:T(1,128)S(1)}) %tuple.32, (bf16[384,4096]{1,0:T(8,128)(2,1)S(1)}, ...), branch_computations={%region_0.4_spmd, %region_4.8_spmd} | conditional | flops 10152052736 | bytes 64452376 | solution.py:86
  46.4 6.3 %fusion.63 = bf16[384,768]{1,0:T(8,128)(2,1)} fusion(bf16[4,4096,768]{2,1,0:T(8,128)(2,1)} %get-tuple-element.25, bf16[384,4096]{1,0:T(8,128)(2,1)S(1)} %get-tuple-element.23, f32[4096]{0:T(1024)S(1)} %bitcast.73, f32[384]{0:T(512)S(1)} %add_rsqrt_fusion.1), kind=kOutput, calls=%fused_computation.65 | convolution fusion | flops 2422505472 | bytes 10044928 | tf_op jit(solution)/shard_map/cond/branch_1_fun/dot_general | solution.py:22
  52.7 2.1 %copy.18 = bf16[384,768]{0,1:T(8,128)(2,1)} copy(bf16[384,768]{1,0:T(8,128)(2,1)} %fusion.63) | data formatting | bytes 1179648 | tf_op jit(solution)/shard_map/cond/branch_1_fun/convert_element_type | solution.py:22
  54.8 6.3 %fusion.66 = bf16[384,768]{1,0:T(8,128)(2,1)} fusion(bf16[4,4096,768]{2,1,0:T(8,128)(2,1)} %get-tuple-element.25, bf16[384,4096]{1,0:T(8,128)(2,1)S(1)} %get-tuple-element.23, f32[4096]{0:T(1024)S(1)} %bitcast.74, f32[384]{0:T(512)S(1)} %add_rsqrt_fusion.1), kind=kOutput, calls=%fused_computation.66 | convolution fusion | flops 2422505472 | bytes 10044928 | tf_op jit(solution)/shard_map/cond/branch_1_fun/dot_general | solution.py:22
  61.0 6.3 %fusion.60 = bf16[384,768]{1,0:T(8,128)(2,1)} fusion(bf16[4,4096,768]{2,1,0:T(8,128)(2,1)} %get-tuple-element.25, bf16[384,4096]{1,0:T(8,128)(2,1)S(1)} %get-tuple-element.23, f32[4096]{0:T(1024)S(1)} %bitcast.75, f32[384]{0:T(512)S(1)} %add_rsqrt_fusion.1), kind=kOutput, calls=%fused_computation.64 | convolution fusion | flops 2422505472 | bytes 10044928 | tf_op jit(solution)/shard_map/cond/branch_1_fun/dot_general | solution.py:22
  67.3 1.4 copy.17
  68.6 1.4 copy.19
  70.0 6.8 %fusion.77 = (f32[12,384]{1,0:T(8,128)S(1)}, f32[12,384,384]{1,2,0:T(8,128)}) fusion(pred[384]{0:T(512)(128)(4,1)S(1)} %iota_compare_fusion.1, bf16[384,12,64]{0,2,1:T(8,128)(2,1)} %bitcast.64, bf16[384,12,64]{0,2,1:T(8,128)(2,1)S(1)} %bitcast.68), kind=kOutput, calls=%fused_computation.84 | convolution fusion | flops 233570688 | bytes 8276352 | tf_op jit(solution)/shard_map/cond/branch_1_fun/sub | solution.py:39
  76.8 3.7 %fusion.59 = bf16[12,64,384]{2,1,0:T(8,128)(2,1)S(1)} fusion(bf16[384,12,64]{0,2,1:T(8,128)(2,1)S(1)} %bitcast.66, f32[12,384,384]{1,2,0:T(8,128)} %get-tuple-element.36, f32[12,384]{1,0:T(8,128)S(1)} %get-tuple-element.35), kind=kOutput, calls=%fused_computation.63 | convolution fusion | flops 230326272 | bytes 8275968 | tf_op jit(solution)/shard_map/cond/branch_1_fun/hqk,khc->qhc/dot_general | solution.py:41
  80.5 7.1 %fusion.42 = bf16[384,4096]{1,0:T(8,128)(2,1)} fusion(bf16[384,768]{0,1:T(8,128)(2,1)S(1)} %bitcast.76, bf16[4,4096,768]{2,1,0:T(8,128)(2,1)} %get-tuple-element.25), kind=kOutput, calls=%fused_computation.46 | convolution fusion | flops 2415919104 | bytes 10027008 | tf_op jit(solution)/shard_map/cond/branch_1_fun/dot_general | solution.py:46
  87.6 1.1 broadcast.57
  89.5 35.7 %all-reduce.2.cloned.1.call-done = bf16[128,4096]{1,0:T(8,128)(2,1)} async-done(((bf16[128,4096]{1,0:T(8,128)(2,1)}), bf16[128,4096]{1,0:T(8,128)(2,1)}) %all-reduce.2.cloned.1.call-update) | async-done | bytes 1048592 | tf_op jit(solution)/shard_map/psum | solution.py:93
  125.2 1.8 add_convert_fusion
  127.0 1.5 collective-permute-start.4
  128.5 37.6 %reduce-scatter.2.cloned.1.call-done = bf16[96,4096]{1,0:T(8,128)(2,1)} async-done(((bf16[384,4096]{1,0:T(8,128)(2,1)}), bf16[96,4096]{1,0:T(8,128)(2,1)}) %reduce-scatter.2.cloned.1.call-update) | async-done | bytes 786448 | tf_op jit(solution)/shard_map/reduce_scatter | solution.py:89
  166.1 1.3 add_convert_fusion.1
  167.5 1.5 collective-permute-start.3
  169.0 20.3 %collective-permute-done.3 = bf16[96,4096]{1,0:T(8,128)(2,1)S(1)} collective-permute-done((bf16[96,4096]{1,0:T(8,128)(2,1)S(1)}, bf16[96,4096]{1,0:T(8,128)(2,1)S(1)}, u32[]{:S(2)}, u32[]{:S(2)}) %collective-permute-start.3) | collective-permute-done | bytes 786464 | tf_op jit(solution)/shard_map/ppermute | solution.py:12
  189.3 0.9 copy.36
  190.2 1.0 copy.37
  (27 shorter events, 4.1 us)
Async XLA Ops:
  7.2 36.8 %copy-start = (bf16[96,4096]{1,0:T(8,128)(2,1)S(1)}, bf16[96,4096]{1,0:T(8,128)(2,1)}, u32[]{:S(2)}) copy-start(bf16[96,4096]{1,0:T(8,128)(2,1)} %param.7) | copy-start | bytes 2359300
  7.2 118.0 %all-reduce.2.cloned.1.call-start = ((), (), s32[]{:S(2)}) async-start(), calls=%async_computation.2 | async-start | bytes 2097152 | tf_op jit(solution)/shard_map/psum | solution.py:93
  7.2 12.3 %collective-permute-start = (bf16[96,4096]{1,0:T(8,128)(2,1)}, bf16[96,4096]{1,0:T(8,128)(2,1)S(1)}, u32[]{:S(2)}, u32[]{:S(2)}) collective-permute-start(bf16[96,4096]{1,0:T(8,128)(2,1)} %param.7), channel_id=1, source_target_pairs={{0,1},{1,2},{2,3},{3,0},{4,5},{5,6},{6,7},{7,4},{8,9},{9,10},{10,1... | collective-permute-start | bytes 2359304 | tf_op jit(solution)/shard_map/ppermute | solution.py:61
  19.6 11.4 %collective-permute-start.1 = (bf16[96,4096]{1,0:T(8,128)(2,1)S(1)}, bf16[96,4096]{1,0:T(8,128)(2,1)S(1)}, u32[]{:S(2)}, u32[]{:S(2)}) collective-permute-start(bf16[96,4096]{1,0:T(8,128)(2,1)S(1)} %collective-permute-done), channel_id=1, source_target_pairs={{0,1},{1,2},{2,3},{3,0},{4,5},{5,6},{6,7},{7,4},{8,9},{9,10},{10,1... | collective-permute-start | bytes 2359304 | tf_op jit(solution)/shard_map/ppermute | solution.py:61
  31.0 11.4 %collective-permute-start.2 = (bf16[96,4096]{1,0:T(8,128)(2,1)S(1)}, bf16[96,4096]{1,0:T(8,128)(2,1)S(1)}, u32[]{:S(2)}, u32[]{:S(2)}) collective-permute-start(bf16[96,4096]{1,0:T(8,128)(2,1)S(1)} %collective-permute-done.1), channel_id=1, source_target_pairs={{0,1},{1,2},{2,3},{3,0},{4,5},{5,6},{6,7},{7,4},{8,9},{9,10},{10,1... | collective-permute-start | bytes 2359304 | tf_op jit(solution)/shard_map/ppermute | solution.py:61
  43.8 1.2 copy-start.2
  43.8 1.2 copy-start.3
  88.7 77.4 %copy-start.1 = (bf16[96,4096]{1,0:T(8,128)(2,1)S(1)}, bf16[96,4096]{1,0:T(8,128)(2,1)}, u32[]{:S(2)}) copy-start(bf16[96,4096]{1,0:T(8,128)(2,1)} %param.7) | copy-start | bytes 2359300
  88.7 77.4 %reduce-scatter.2.cloned.1.call-start = ((), (), s32[]{:S(2)}) async-start(), calls=%async_computation.1 | async-start | bytes 3932160 | tf_op jit(solution)/shard_map/reduce_scatter | solution.py:89
  127.0 42.0 %collective-permute-start.4 = (bf16[128,4096]{1,0:T(8,128)(2,1)S(1)}, bf16[128,4096]{1,0:T(8,128)(2,1)S(1)}, u32[]{:S(2)}, u32[]{:S(2)}) collective-permute-start(bf16[128,4096]{1,0:T(8,128)(2,1)S(1)} %add_convert_fusion), channel_id=1, source_target_pairs={{0,4},{4,8},{8,12},{12,16},{16,20},{20,24},{24,28},{28,0},{1,5},{5... | collective-permute-start | bytes 3145736 | tf_op jit(solution)/shard_map/ppermute | solution.py:12
  167.5 21.9 %collective-permute-start.3 = (bf16[96,4096]{1,0:T(8,128)(2,1)S(1)}, bf16[96,4096]{1,0:T(8,128)(2,1)S(1)}, u32[]{:S(2)}, u32[]{:S(2)}) collective-permute-start(bf16[96,4096]{1,0:T(8,128)(2,1)S(1)} %add_convert_fusion.1), channel_id=1, source_target_pairs={{0,4},{4,8},{8,12},{12,16},{16,20},{20,24},{24,28},{28,0},{1,5},{5... | collective-permute-start | bytes 2359304 | tf_op jit(solution)/shard_map/ppermute | solution.py:12
Sparse Core Ops, SparseCore 0:
  88.8 36.3 all-reduce.1
  127.7 38.3 reduce-scatter.1
